TPU v7x, 32 devices: a whole 2x2x4 slice. The times are simulated.
32 devices in a mesh: fsdp: 4 (over y, x), tp: 8 (over z, core).
Axes of the slice: x: 2, y: 2, z: 4, core: 2. Of those that a mesh axis runs over, the one named last changes fastest.
Arguments:
- ref_gate: bfloat16 [3072, 11008], P('fsdp', 'tp'), may hold values from -6 to 6
- ref_up: bfloat16 [3072, 11008], P('fsdp', 'tp'), may hold values from -6 to 6
- ref_residual: bfloat16 [3072, 4096], P('fsdp', 'tp'), may hold values from -6 to 6
- ref_modality: int32 [3072], P('fsdp'), may hold values 0 or 1
- ref_down_text: bfloat16 [4096, 11008], P('fsdp', 'tp'), may hold values from -0.0546875 to 0.0546875
- ref_down_image: bfloat16 [4096, 11008], P('fsdp', 'tp'), may hold values from -0.0546875 to 0.0546875
- pol_gate: bfloat16 [3072, 11008], P('fsdp', 'tp'), may hold values from -6 to 6
- pol_up: bfloat16 [3072, 11008], P('fsdp', 'tp'), may hold values from -6 to 6
- pol_modality: int32 [3072], P('fsdp'), may hold values 0 or 1
- pol_segment: int32 [3072], P('fsdp'), may hold values from 0 to 5, never falling along the last dimension, each value on 1 to 768 neighbouring positions
- pair_margin: float32 [3], replicated, may hold values from -30 to 30
- token_cotangent: bfloat16 [3072, 4096], P('fsdp', 'tp'), may hold values from -24 to 24
- pol_down_text: bfloat16 [4096, 11008], P('fsdp', 'tp'), may hold values from -0.0546875 to 0.0546875
- pol_down_image: bfloat16 [4096, 11008], P('fsdp', 'tp'), may hold values from -0.0546875 to 0.0546875
Outputs:
- ref_out: bfloat16 [3072, 4096], P('fsdp', 'tp')
- grad_gate: bfloat16 [3072, 11008], P('fsdp', 'tp')
- grad_up: bfloat16 [3072, 11008], P('fsdp', 'tp')
- grad_down_text: float32 [4096, 11008], P('fsdp', 'tp')
- grad_down_image: float32 [4096, 11008], P('fsdp', 'tp')
Inputs may be any that keep to these rules, and one draw needn't show every extreme that they name: `ref_modality`: 0 marks a text token, 1 an image token. `pol_modality`: 0 marks a text token, 1 an image token. `pol_segment`: response numbers never fall along the tokens; responses 2p and 2p + 1 are the chosen and the rejected response of pair p; every response has at least one token.
All inputs are finite; a program needn't handle non-finite values. No bound on the sum of `ref_modality` or of `pol_modality` on one device may be relied on, other than what follows from the above.
Results may differ from a plain program's by a relative error of at most 0.015.
Values may be sent and summed in bfloat16 or wider, within the bound.
A program may use at most 192 MiB of HBM per device.

v0:
```python
import jax
import jax.numpy as jnp
from jax import lax
from jax.sharding import PartitionSpec as P

dpo_beta = 0.1


def split_hidden(gate, up, modality):
    gate_f = gate.astype(jnp.float32)
    up_f = up.astype(jnp.float32)
    sig = jax.nn.sigmoid(gate_f)
    act = gate_f * sig
    hidden = (act * up_f).astype(jnp.bfloat16)
    image = (modality == 1)[:, None]
    zero = jnp.zeros_like(hidden)
    return (jnp.where(image, zero, hidden), jnp.where(image, hidden, zero), gate_f, up_f, sig, act)


def forward_term(left_text, left_image, right_text, right_image):
    contract = (((1,), (1,)), ((), ()))
    part = lax.dot_general(left_text, right_text, contract, preferred_element_type=jnp.float32)
    return part + lax.dot_general(
        left_image, right_image, contract, preferred_element_type=jnp.float32
    )


def backward_term(left_text, left_image, right_text, right_image):
    part = jnp.dot(left_text, right_text, preferred_element_type=jnp.float32)
    return part + jnp.dot(left_image, right_image, preferred_element_type=jnp.float32)


def per_device(
    ref_gate,
    ref_up,
    ref_residual,
    ref_modality,
    ref_down_text,
    ref_down_image,
    pol_gate,
    pol_up,
    pol_modality,
    pol_segment,
    pair_margin,
    token_cotangent,
    pol_down_text,
    pol_down_image,
):
    ref_text, ref_image, _, _, _, _ = split_hidden(ref_gate, ref_up, ref_modality)
    pol_text, pol_image, gate_f, up_f, sig, act = split_hidden(pol_gate, pol_up, pol_modality)
    seg_ids = jnp.arange(2 * pair_margin.shape[0], dtype=jnp.int32)
    pair_weight = dpo_beta * jax.nn.sigmoid(-dpo_beta * pair_margin)
    table = jnp.repeat(pair_weight, 2) * jnp.where(seg_ids % 2 == 0, -1.0, 1.0).astype(jnp.float32)
    coef = jnp.sum(
        jnp.where(pol_segment[:, None] == seg_ids[None, :], table[None, :], jnp.float32(0.0)),
        axis=1,
    )
    local_cot = (coef[:, None] * token_cotangent.astype(jnp.float32)).astype(jnp.bfloat16)
    full_cot = lax.all_gather(local_cot, "tp", axis=1, tiled=True)
    image_p = (pol_modality == 1)[:, None]
    zero_cot = jnp.zeros_like(full_cot)
    cot_text = jnp.where(image_p, zero_cot, full_cot)
    cot_image = jnp.where(image_p, full_cot, zero_cot)
    stacked_ref = jnp.stack([ref_down_text, ref_down_image])
    piece = lax.all_gather(stacked_ref, "fsdp", axis=1, tiled=True)
    terms = forward_term(ref_text, ref_image, piece[0], piece[1])
    d_hidden = backward_term(
        cot_text,
        cot_image,
        lax.all_gather(pol_down_text, "fsdp", axis=0, tiled=True),
        lax.all_gather(pol_down_image, "fsdp", axis=0, tiled=True),
    )
    summed = lax.psum_scatter(
        terms.astype(jnp.bfloat16), "tp", scatter_dimension=1, tiled=True
    ).astype(jnp.float32)
    ref_out = (summed + ref_residual.astype(jnp.float32)).astype(jnp.bfloat16)
    grad_gate = (d_hidden * up_f * sig * (1.0 + gate_f * (1.0 - sig))).astype(jnp.bfloat16)
    grad_up = (d_hidden * act).astype(jnp.bfloat16)
    width = pol_down_text.shape[1]
    over_rows = (((0,), (0,)), ((), ()))
    term_text = lax.dot_general(cot_text, pol_text, over_rows, preferred_element_type=jnp.float32)
    term_image = lax.dot_general(
        cot_image, pol_image, over_rows, preferred_element_type=jnp.float32
    )
    grads = lax.psum_scatter(
        jnp.concatenate([term_text, term_image], axis=1).astype(jnp.bfloat16),
        "fsdp",
        scatter_dimension=0,
        tiled=True,
    ).astype(jnp.float32)
    return (ref_out, grad_gate, grad_up, grads[:, :width], grads[:, width:])


def solution(mesh):
    in_specs = (
        P("fsdp", "tp"),
        P("fsdp", "tp"),
        P("fsdp", "tp"),
        P("fsdp"),
        P("fsdp", "tp"),
        P("fsdp", "tp"),
        P("fsdp", "tp"),
        P("fsdp", "tp"),
        P("fsdp"),
        P("fsdp"),
        P(),
        P("fsdp", "tp"),
        P("fsdp", "tp"),
        P("fsdp", "tp"),
    )
    out_specs = (
        P("fsdp", "tp"),
        P("fsdp", "tp"),
        P("fsdp", "tp"),
        P("fsdp", "tp"),
        P("fsdp", "tp"),
    )
    return jax.shard_map(
        per_device, mesh=mesh, in_specs=in_specs, out_specs=out_specs, check_vma=False
    )
```

profile of v0, /device:TPU:0, one launch (start us, length us, event | category | flops | bytes accessed | tf_op | source)
XLA Modules:
  0.0 803.0 jit_solution(6594723527638454698)
XLA Ops:
  7.2 0.0 all-gather.5.cloned.1.call-start
  7.2 5.7 pad_maximum_fusion.1
  12.9 0.0 copy-start.10
  12.9 0.0 copy-start.4
  12.9 0.0 copy-start
  12.9 0.0 all-gather.5.cloned.1.call-update
  12.9 0.0 copy-start.2
  12.9 0.0 copy-start.6
  12.9 0.0 all-gather.7.cloned.1.call-start
  13.0 0.6 copy-done.10
  13.5 0.1 broadcast_in_dim.66
  13.6 0.1 reshape.33
  13.7 0.0 copy-done.4
  13.7 0.1 select_reduce_fusion
  13.8 0.2 copy-done
  14.0 1.1 multiply_convert_fusion.1
  15.1 0.0 all-gather.7.cloned.1.call-update
  15.2 0.0 all-gather.9.cloned.1.call-start
  15.2 0.7 all-gather.9.cloned.1.call-update
  15.9 0.0 all-gather.11.cloned.1.call-start
  15.9 0.5 all-gather.11.cloned.1.call-update
  16.5 0.0 reduce-scatter.3.cloned.1.call-start
  16.5 0.0 copy-done.2
  16.5 205.2 %all-gather.5.cloned.1.call-done = bf16[2,4096,1376]{1,2,0:T(8,128)(2,1)} async-done(((bf16[2,1024,1376]{1,2,0:T(8,128)(2,1)}), bf16[2,4096,1376]{1,2,0:T(8,128)(2,1)}) %all-gather.5.cloned.1.call-update) | async-done | bytes 22544400 | tf_op jit(solution)/shard_map/all_gather | solution.py:65
  221.8 0.0 copy-done.6
  221.8 0.0 copy-start.7
  221.8 18.6 %fusion = f32[768,4096]{1,0:T(8,128)} fusion(bf16[2,4096,1376]{1,2,0:T(8,128)(2,1)} %all-gather.5.cloned.1.call-done, pred[768]{0:T(1024)(128)(4,1)S(1)} %broadcast_compare_fusion.1, bf16[768,1376]{0,1:T(8,128)(2,1)S(1)} %copy-done.6, bf16[768,1376]{0,1:T(8,128)(2,1)} %param.14), kind=kOutput, calls=%fused_computation.5 | convolution fusion | flops 8666554368 | bytes 28082944 | tf_op jit(solution)/shard_map/dot_general | solution.py:23
  240.3 0.0 copy-done.7
  240.3 18.3 %add_convert_fusion = bf16[768,4096]{1,0:T(8,128)(2,1)} fusion(f32[768,4096]{1,0:T(8,128)} %fusion, bf16[2,4096,1376]{1,2,0:T(8,128)(2,1)} %all-gather.5.cloned.1.call-done, pred[768]{0:T(1024)(128)(4,1)S(1)} %broadcast_compare_fusion.1, bf16[768,1376]{0,1:T(8,128)(2,1)S(1)} %copy-done.6, bf16[768,1376]{0,1:T(8,128)(2,1)S(1)} %copy-done.7), kind=kOutput, calls=%fused_computation.3 | convolution fusion | flops 8672845824 | bytes 34374400 | tf_op jit(solution)/shard_map/dot_general | solution.py:22
  258.7 0.0 copy-start.3
  258.7 0.0 copy-start.8
  258.7 0.0 reduce-scatter.3.cloned.1.call-update
  258.7 0.2 reduce-scatter.5.cloned.1.call-start
  258.9 0.4 copy-done.3
  259.4 29.3 %all-gather.7.cloned.1.call-done = bf16[768,4096]{1,0:T(8,128)(2,1)} async-done(((bf16[768,512]{1,0:T(8,128)(2,1)}), bf16[768,4096]{1,0:T(8,128)(2,1)}) %all-gather.7.cloned.1.call-update) | async-done | bytes 6291472 | tf_op jit(solution)/shard_map/all_gather | solution.py:59
  288.7 0.0 copy-done.8
  288.7 0.0 copy-start.5
  288.7 0.0 copy-start.9
  288.7 15.3 %convolution_convert_fusion = bf16[4096,1376]{0,1:T(8,128)(2,1)} fusion(bf16[768,4096]{1,0:T(8,128)(2,1)} %all-gather.7.cloned.1.call-done, pred[768]{0:T(1024)(128)(4,1)S(1)} %broadcast_compare_fusion, bf16[768,1376]{0,1:T(8,128)(2,1)} %param.21, bf16[768,1376]{0,1:T(8,128)(2,1)S(1)} %copy-done.8), kind=kOutput, calls=%fused_computation.1 | convolution fusion | flops 8675336192 | bytes 21791488 | tf_op jit(solution)/shard_map/dot_general | solution.py:82
  304.0 0.0 copy-done.5
  304.0 0.0 copy-done.9
  304.0 12.3 %convolution_convert_fusion.1 = bf16[4096,1376]{0,1:T(8,128)(2,1)} fusion(bf16[768,4096]{1,0:T(8,128)(2,1)S(1)} %copy-done.5, pred[768]{0:T(1024)(128)(4,1)S(1)} %broadcast_compare_fusion, bf16[768,1376]{0,1:T(8,128)(2,1)S(1)} %copy-done.9, bf16[768,1376]{0,1:T(8,128)(2,1)S(1)} %copy-done.8), kind=kOutput, calls=%fused_computation.2 | convolution fusion | flops 8675336192 | bytes 21791488 | tf_op jit(solution)/shard_map/dot_general | solution.py:81
  316.3 20.2 %pad_maximum_fusion = bf16[4096,2752]{0,1:T(8,128)(2,1)} fusion(bf16[4096,1376]{0,1:T(8,128)(2,1)} %convolution_convert_fusion, bf16[4096,1376]{0,1:T(8,128)(2,1)} %convolution_convert_fusion.1), kind=kLoop, calls=%fused_computation | loop fusion | flops 45088768 | bytes 45088768 | tf_op jit(solution)/shard_map/concatenate | solution.py:86
  336.4 0.0 reduce-scatter.5.cloned.1.call-update
  336.4 64.2 %all-gather.9.cloned.1.call-done = bf16[4096,1376]{0,1:T(8,128)(2,1)} async-done(((bf16[1024,1376]{0,1:T(8,128)(2,1)}), bf16[4096,1376]{0,1:T(8,128)(2,1)}) %all-gather.9.cloned.1.call-update) | async-done | bytes 11272208 | tf_op jit(solution)/shard_map/all_gather | solution.py:70
  400.7 15.1 %fusion.15 = f32[768,1376]{0,1:T(8,128)} fusion(bf16[4096,1376]{0,1:T(8,128)(2,1)} %all-gather.9.cloned.1.call-done, bf16[768,4096]{1,0:T(8,128)(2,1)} %all-gather.7.cloned.1.call-done, pred[768]{0:T(1024)(128)(4,1)S(1)} %broadcast_compare_fusion), kind=kOutput, calls=%fused_computation.33 | convolution fusion | flops 8660189184 | bytes 21791488 | tf_op jit(solution)/shard_map/dot_general | solution.py:29
  415.8 0.0 copy-start.1
  415.8 98.1 %all-gather.11.cloned.1.call-done = bf16[4096,1376]{0,1:T(8,128)(2,1)} async-done(((bf16[1024,1376]{0,1:T(8,128)(2,1)}), bf16[4096,1376]{0,1:T(8,128)(2,1)}) %all-gather.11.cloned.1.call-update) | async-done | bytes 11272208 | tf_op jit(solution)/shard_map/all_gather | solution.py:71
  513.9 17.5 %multiply_convert_fusion = (bf16[768,1376]{0,1:T(8,128)(2,1)}, bf16[768,1376]{0,1:T(8,128)(2,1)}) fusion(bf16[768,1376]{0,1:T(8,128)(2,1)S(1)} %copy-done.8, bf16[768,1376]{0,1:T(8,128)(2,1)} %param.21, f32[768,1376]{0,1:T(8,128)} %fusion.15, bf16[4096,1376]{0,1:T(8,128)(2,1)} %all-gather.11.cloned.1.call-done, ...), kind=kOutput, calls=%fused_computation.30 | convolution fusion | flops 8677097472 | bytes 30245632 | tf_op jit(solution)/shard_map/dot_general | solution.py:30
  531.4 54.4 %reduce-scatter.3.cloned.1.call-done = bf16[768,512]{1,0:T(8,128)(2,1)} async-done(((bf16[768,4096]{1,0:T(8,128)(2,1)}), bf16[768,512]{1,0:T(8,128)(2,1)}) %reduce-scatter.3.cloned.1.call-update) | async-done | bytes 786448 | tf_op jit(solution)/shard_map/reduce_scatter | solution.py:73
  585.8 0.0 copy-done.1
  585.8 2.2 add_convert_fusion.1
  588.0 199.8 %reduce-scatter.5.cloned.1.call-done = bf16[1024,2752]{0,1:T(8,128)(2,1)} async-done(((bf16[4096,2752]{0,1:T(8,128)(2,1)}), bf16[1024,2752]{0,1:T(8,128)(2,1)}) %reduce-scatter.5.cloned.1.call-update) | async-done | bytes 5636112 | tf_op jit(solution)/shard_map/reduce_scatter | solution.py:85
  787.8 8.3 %fusion.39 = (f32[1024,1376]{0,1:T(8,128)}, f32[1024,1376]{0,1:T(8,128)}) fusion(bf16[1024,2752]{0,1:T(8,128)(2,1)} %reduce-scatter.5.cloned.1.call-done), kind=kLoop, calls=%fused_computation.62 | loop fusion | bytes 22544384 | tf_op jit(solution)/shard_map/slice | solution.py:91
  (4 shorter events, 0.0 us)
Async XLA Ops:
  7.2 214.6 %all-gather.5.cloned.1.call-start = ((), (), s32[]{:S(2)}) async-start(), calls=%async_computation.2 | async-start | bytes 28180480 | tf_op jit(solution)/shard_map/all_gather | solution.py:65
  12.9 0.7 copy-start.10
  12.9 0.8 copy-start.4
  12.9 1.2 copy-start
  12.9 3.6 copy-start.2
  12.9 208.9 %copy-start.6 = (bf16[768,1376]{0,1:T(8,128)(2,1)S(1)}, bf16[768,1376]{0,1:T(8,128)(2,1)}, u32[]{:S(2)}) copy-start(bf16[768,1376]{0,1:T(8,128)(2,1)} %param.15) | copy-start | bytes 6340612
  12.9 275.8 %all-gather.7.cloned.1.call-start = ((), (), s32[]{:S(2)}) async-start(), calls=%async_computation.4 | async-start | bytes 7077888 | tf_op jit(solution)/shard_map/all_gather | solution.py:59
  15.2 385.5 %all-gather.9.cloned.1.call-start = ((), (), s32[]{:S(2)}) async-start(), calls=%async_computation.5 | async-start | bytes 14090240 | tf_op jit(solution)/shard_map/all_gather | solution.py:70
  15.9 498.0 %all-gather.11.cloned.1.call-start = ((), (), s32[]{:S(2)}) async-start(), calls=%async_computation.6 | async-start | bytes 14090240 | tf_op jit(solution)/shard_map/all_gather | solution.py:71
  16.5 569.3 %reduce-scatter.3.cloned.1.call-start = ((), (), s32[]{:S(2)}) async-start(), calls=%async_computation.3 | async-start | bytes 7077888 | tf_op jit(solution)/shard_map/reduce_scatter | solution.py:73
  221.8 18.6 %copy-start.7 = (bf16[768,1376]{0,1:T(8,128)(2,1)S(1)}, bf16[768,1376]{0,1:T(8,128)(2,1)}, u32[]{:S(2)}) copy-start(bf16[768,1376]{0,1:T(8,128)(2,1)} %param.14) | copy-start | bytes 6340612
  258.7 0.7 copy-start.3
  258.7 30.0 %copy-start.8 = (bf16[768,1376]{0,1:T(8,128)(2,1)S(1)}, bf16[768,1376]{0,1:T(8,128)(2,1)}, u32[]{:S(2)}) copy-start(bf16[768,1376]{0,1:T(8,128)(2,1)} %param.20) | copy-start | bytes 6340612
  258.7 529.1 %reduce-scatter.5.cloned.1.call-start = ((), (), s32[]{:S(2)}) async-start(), calls=%async_computation.7 | async-start | bytes 28180480 | tf_op jit(solution)/shard_map/reduce_scatter | solution.py:85
  288.7 15.3 %copy-start.5 = (bf16[768,4096]{1,0:T(8,128)(2,1)S(1)}, bf16[768,4096]{1,0:T(8,128)(2,1)}, u32[]{:S(2)}) copy-start(bf16[768,4096]{1,0:T(8,128)(2,1)} %all-gather.7.cloned.1.call-done) | copy-start | bytes 18874372
  288.7 15.3 %copy-start.9 = (bf16[768,1376]{0,1:T(8,128)(2,1)S(1)}, bf16[768,1376]{0,1:T(8,128)(2,1)}, u32[]{:S(2)}) copy-start(bf16[768,1376]{0,1:T(8,128)(2,1)} %param.21) | copy-start | bytes 6340612
  415.8 170.1 %copy-start.1 = (bf16[768,512]{1,0:T(8,128)(2,1)S(1)}, bf16[768,512]{1,0:T(8,128)(2,1)}, u32[]{:S(2)}) copy-start(bf16[768,512]{1,0:T(8,128)(2,1)} %param.16) | copy-start | bytes 2359300
Sparse Core Ops, SparseCore 0:
  13.0 208.7 all-gather.4
  224.0 64.6 all-gather.6
  290.5 110.1 all-gather.8
  402.4 111.4 all-gather.10
  516.0 69.7 reduce-scatter.2
  588.8 198.9 reduce-scatter.4
where the time goes:
time: 803 us
  waiting for transfers between devices  652 us (81%)
  matrix products  97 us (12%)
  other arithmetic  29.2 us (4%)
  between operations  14.2 us (2%)
  local copies, waits for them, and re-layouts  9.76 us (1%)
    all_gather x1, waiting for transfers between devices, per_device(): piece = lax.all_gather(stacked_ref, 'fsdp', axis=1, tiled=True)  205 us
    reduce_scatter x1, waiting for transfers between devices, per_device(): lax.psum_scatter(jnp.concatenate([term_text, term_image], axis=1).astype(...  200 us
    all_gather x1, waiting for transfers between devices, per_device(): lax.all_gather(pol_down_image, 'fsdp', axis=0, tiled=True)  98.1 us
    all_gather x1, waiting for transfers between devices, per_device(): lax.all_gather(pol_down_text, 'fsdp', axis=0, tiled=True)  64.2 us
    reduce_scatter x1, waiting for transfers between devices, per_device(): lax.psum_scatter(terms.astype(jnp.bfloat16), 'tp', scatter_dimension=1, t...  54.4 us
    all_gather x1, waiting for transfers between devices, per_device(): full_cot = lax.all_gather(local_cot, 'tp', axis=1, tiled=True)  29.3 us
    concatenate x1, other arithmetic, per_device(): jnp.concatenate([term_text, term_image], axis=1).astype(jnp.bfloat16)  20.2 us
    dot_general x1, matrix products, forward_term(): lax.dot_general(left_image, right_image, contract, preferred_element_type...  18.6 us
  transfers between devices with their start and end apart: 6, of which 6 were waited for; matrix products, arithmetic and copies ran while one was open for 15% of the time, Pallas kernels for 0%

commit v1 on v0

--- a/solution.py
+++ b/solution.py
@@ -62,7 +62,7 @@
     cot_text = jnp.where(image_p, zero_cot, full_cot)
     cot_image = jnp.where(image_p, full_cot, zero_cot)
     stacked_ref = jnp.stack([ref_down_text, ref_down_image])
-    piece = lax.all_gather(stacked_ref, "fsdp", axis=1, tiled=True)
+    piece = jnp.concatenate(lax.all_gather(stacked_ref, axis_name="fsdp"), 1)
     terms = forward_term(ref_text, ref_image, piece[0], piece[1])
     d_hidden = backward_term(
         cot_text,

time: 803 us -> 804 us (level)
  local copies, waits for them, and re-layouts: 9.76 us -> 53.3 us
  waiting for transfers between devices: 652 us -> 612 us
    all_gather x1, waiting for transfers between devices: 29.3 us -> 0.01 us  [per_device(): full_cot = lax.all_gather(local_cot, 'tp', axis=1, tiled=True)]
    all_gather x0 -> x1, local copies, waits for them, and re-layouts: none -> 29.3 us  [per_device(): piece = jnp.concatenate(lax.all_gather(stacked_ref, axis_name='fsdp'), 1)]
    slice x0 -> x1, local copies, waits for them, and re-layouts: none -> 12.8 us  [per_device(): terms = forward_term(ref_text, ref_image, piece[0], piece[1])]
    all_gather x1, waiting for transfers between devices: 64.2 us -> 53.4 us  [per_device(): lax.all_gather(pol_down_text, 'fsdp', axis=0, tiled=True)]
  transfers between devices with their start and end apart: 6 -> 6, of which waited for: 6 -> 5; matrix products, arithmetic and copies ran while one was open for 15% -> 20% of each run, Pallas kernels for 0% -> 0%
where the time goes in v1:
time: 804 us; the launch traced here: 803 us
  waiting for transfers between devices  612 us (76%)
  matrix products  93.7 us (12%)
  local copies, waits for them, and re-layouts  53.3 us (7%)
  other arithmetic  29.2 us (4%)
  between operations  14.2 us (2%)
    all_gather x1, waiting for transfers between devices, per_device(): piece = jnp.concatenate(lax.all_gather(stacked_ref, axis_name='fsdp'), 1)  205 us
    reduce_scatter x1, waiting for transfers between devices, per_device(): lax.psum_scatter(jnp.concatenate([term_text, term_image], axis=1).astype(...  200 us
    all_gather x1, waiting for transfers between devices, per_device(): lax.all_gather(pol_down_image, 'fsdp', axis=0, tiled=True)  98.1 us
    reduce_scatter x1, waiting for transfers between devices, per_device(): lax.psum_scatter(terms.astype(jnp.bfloat16), 'tp', scatter_dimension=1, t...  54.4 us
    all_gather x1, waiting for transfers between devices, per_device(): lax.all_gather(pol_down_text, 'fsdp', axis=0, tiled=True)  53.4 us
    all_gather x1, local copies, waits for them, and re-layouts, per_device(): piece = jnp.concatenate(lax.all_gather(stacked_ref, axis_name='fsdp'), 1)  29.3 us
    concatenate x1, other arithmetic, per_device(): jnp.concatenate([term_text, term_image], axis=1).astype(jnp.bfloat16)  20.1 us
    dot_general x1, matrix products, forward_term(): lax.dot_general(left_image, right_image, contract, preferred_element_type...  18.3 us
  transfers between devices with their start and end apart: 6, of which 5 were waited for; matrix products, arithmetic and copies ran while one was open for 20% of the time, Pallas kernels for 0%

profile of v1, /device:TPU:0, one launch (start us, length us, event | category | flops | bytes accessed | tf_op | source)
XLA Modules:
  0.0 803.0 jit_solution(17811932397686291448)
XLA Ops:
  7.2 0.0 all-gather.12.cloned.1.call-start
  7.2 5.7 pad_maximum_fusion.1
  12.9 0.0 copy-start.9
  12.9 0.0 copy-start.4
  12.9 0.0 copy-start
  12.9 0.0 all-gather.12.cloned.1.call-update
  12.9 0.0 copy-start.2
  12.9 0.0 all-gather.6.cloned.1.call-start
  13.0 0.6 copy-done.9
  13.5 0.1 broadcast_in_dim.66
  13.6 0.1 reshape.42
  13.7 0.0 copy-done.4
  13.7 0.1 select_reduce_fusion
  13.8 0.2 copy-done
  14.0 1.1 multiply_convert_fusion.1
  15.1 0.0 all-gather.6.cloned.1.call-update
  15.2 0.0 all-gather.8.cloned.1.call-start
  15.2 0.7 all-gather.8.cloned.1.call-update
  15.9 0.0 all-gather.10.cloned.1.call-start
  15.9 0.5 all-gather.10.cloned.1.call-update
  16.5 0.0 reduce-scatter.3.cloned.1.call-start
  16.5 0.0 copy-done.2
  16.5 205.2 %all-gather.12.cloned.1.call-done = bf16[8,1024,1376]{1,2,0:T(8,128)(2,1)} async-done(((bf16[2,1024,1376]{1,2,0:T(8,128)(2,1)}), bf16[8,1024,1376]{1,2,0:T(8,128)(2,1)}) %all-gather.12.cloned.1.call-update) | async-done | bytes 22544400 | tf_op jit(solution)/shard_map/all_gather | solution.py:65
  221.8 29.3 %copy.21 = bf16[4,2,1024,1376]{3,2,0,1:T(8,128)(2,1)} copy(bf16[4,2,1024,1376]{2,3,1,0:T(8,128)(2,1)} %bitcast.11) | data formatting | bytes 45088768 | tf_op jit(solution)/shard_map/all_gather | solution.py:65
  251.0 0.0 copy-start.6
  251.0 12.8 %fusion.38 = (bf16[1,4,1024,1376]{3,2,1,0:T(8,128)(2,1)}, bf16[1,4,1024,1376]{3,2,1,0:T(8,128)(2,1)S(1)}) fusion(bf16[2,4,1024,1376]{3,2,1,0:T(8,128)(2,1)} %bitcast.10), kind=kLoop, calls=%fused_computation.59 | loop fusion | bytes 45088768 | tf_op jit(solution)/shard_map/slice | solution.py:66
  263.8 0.0 copy-done.6
  263.8 14.2 %fusion.17 = f32[768,4096]{1,0:T(8,128)} fusion(bf16[4096,1376]{1,0:T(8,128)(2,1)S(1)} %bitcast.13, pred[768]{0:T(1024)(128)(4,1)S(1)} %broadcast_compare_fusion.1, bf16[768,1376]{0,1:T(8,128)(2,1)S(1)} %copy-done.6, bf16[768,1376]{0,1:T(8,128)(2,1)} %param.14), kind=kOutput, calls=%fused_computation.33 | convolution fusion | flops 8666554368 | bytes 28082944 | tf_op jit(solution)/shard_map/dot_general | solution.py:22
  278.0 18.3 %add_convert_fusion = bf16[768,4096]{1,0:T(8,128)(2,1)} fusion(f32[768,4096]{1,0:T(8,128)} %fusion.17, bf16[4096,1376]{1,0:T(8,128)(2,1)} %bitcast.12, pred[768]{0:T(1024)(128)(4,1)S(1)} %broadcast_compare_fusion.1, bf16[768,1376]{0,1:T(8,128)(2,1)S(1)} %copy-done.6, bf16[768,1376]{0,1:T(8,128)(2,1)} %param.14), kind=kOutput, calls=%fused_computation.3 | convolution fusion | flops 8672845824 | bytes 34374400 | tf_op jit(solution)/shard_map/dot_general | solution.py:23
  296.3 0.0 copy-start.3
  296.4 0.0 copy-start.7
  296.4 0.0 reduce-scatter.3.cloned.1.call-update
  296.4 0.2 reduce-scatter.5.cloned.1.call-start
  296.6 0.4 copy-done.3
  297.0 0.0 all-gather.6.cloned.1.call-done
  297.1 1.4 copy-done.7
  298.5 0.0 copy-start.5
  298.5 0.0 copy-start.8
  298.5 16.4 %convolution_convert_fusion = bf16[4096,1376]{0,1:T(8,128)(2,1)} fusion(bf16[768,4096]{1,0:T(8,128)(2,1)} %all-gather.6.cloned.1.call-done, pred[768]{0:T(1024)(128)(4,1)S(1)} %broadcast_compare_fusion, bf16[768,1376]{0,1:T(8,128)(2,1)} %param.21, bf16[768,1376]{0,1:T(8,128)(2,1)S(1)} %copy-done.7), kind=kOutput, calls=%fused_computation.1 | convolution fusion | flops 8675336192 | bytes 21791488 | tf_op jit(solution)/shard_map/dot_general | solution.py:82
  314.9 0.0 copy-done.5
  314.9 0.0 copy-done.8
  314.9 12.2 %convolution_convert_fusion.1 = bf16[4096,1376]{0,1:T(8,128)(2,1)} fusion(bf16[768,4096]{1,0:T(8,128)(2,1)S(1)} %copy-done.5, pred[768]{0:T(1024)(128)(4,1)S(1)} %broadcast_compare_fusion, bf16[768,1376]{0,1:T(8,128)(2,1)S(1)} %copy-done.8, bf16[768,1376]{0,1:T(8,128)(2,1)S(1)} %copy-done.7), kind=kOutput, calls=%fused_computation.2 | convolution fusion | flops 8675336192 | bytes 21791488 | tf_op jit(solution)/shard_map/dot_general | solution.py:81
  327.2 20.1 %pad_maximum_fusion = bf16[4096,2752]{0,1:T(8,128)(2,1)} fusion(bf16[4096,1376]{0,1:T(8,128)(2,1)} %convolution_convert_fusion, bf16[4096,1376]{0,1:T(8,128)(2,1)} %convolution_convert_fusion.1), kind=kLoop, calls=%fused_computation | loop fusion | flops 45088768 | bytes 45088768 | tf_op jit(solution)/shard_map/concatenate | solution.py:86
  347.3 0.0 reduce-scatter.5.cloned.1.call-update
  347.3 53.4 %all-gather.8.cloned.1.call-done = bf16[4096,1376]{0,1:T(8,128)(2,1)} async-done(((bf16[1024,1376]{0,1:T(8,128)(2,1)}), bf16[4096,1376]{0,1:T(8,128)(2,1)}) %all-gather.8.cloned.1.call-update) | async-done | bytes 11272208 | tf_op jit(solution)/shard_map/all_gather | solution.py:70
  400.7 15.1 %fusion.13 = f32[768,1376]{0,1:T(8,128)} fusion(bf16[4096,1376]{0,1:T(8,128)(2,1)} %all-gather.8.cloned.1.call-done, bf16[768,4096]{1,0:T(8,128)(2,1)} %all-gather.6.cloned.1.call-done, pred[768]{0:T(1024)(128)(4,1)S(1)} %broadcast_compare_fusion), kind=kOutput, calls=%fused_computation.29 | convolution fusion | flops 8660189184 | bytes 21791488 | tf_op jit(solution)/shard_map/dot_general | solution.py:29
  415.8 0.0 copy-start.1
  415.8 98.1 %all-gather.10.cloned.1.call-done = bf16[4096,1376]{0,1:T(8,128)(2,1)} async-done(((bf16[1024,1376]{0,1:T(8,128)(2,1)}), bf16[4096,1376]{0,1:T(8,128)(2,1)}) %all-gather.10.cloned.1.call-update) | async-done | bytes 11272208 | tf_op jit(solution)/shard_map/all_gather | solution.py:71
  513.9 17.5 %multiply_convert_fusion = (bf16[768,1376]{0,1:T(8,128)(2,1)}, bf16[768,1376]{0,1:T(8,128)(2,1)}) fusion(bf16[768,1376]{0,1:T(8,128)(2,1)S(1)} %copy-done.7, bf16[768,1376]{0,1:T(8,128)(2,1)} %param.21, f32[768,1376]{0,1:T(8,128)} %fusion.13, bf16[4096,1376]{0,1:T(8,128)(2,1)} %all-gather.10.cloned.1.call-done, ...), kind=kOutput, calls=%fused_computation.26 | convolution fusion | flops 8677097472 | bytes 30245632 | tf_op jit(solution)/shard_map/dot_general | solution.py:30
  531.4 54.4 %reduce-scatter.3.cloned.1.call-done = bf16[768,512]{1,0:T(8,128)(2,1)} async-done(((bf16[768,4096]{1,0:T(8,128)(2,1)}), bf16[768,512]{1,0:T(8,128)(2,1)}) %reduce-scatter.3.cloned.1.call-update) | async-done | bytes 786448 | tf_op jit(solution)/shard_map/reduce_scatter | solution.py:73
  585.8 0.0 copy-done.1
  585.8 2.2 add_convert_fusion.1
  588.0 199.8 %reduce-scatter.5.cloned.1.call-done = bf16[1024,2752]{0,1:T(8,128)(2,1)} async-done(((bf16[4096,2752]{0,1:T(8,128)(2,1)}), bf16[1024,2752]{0,1:T(8,128)(2,1)}) %reduce-scatter.5.cloned.1.call-update) | async-done | bytes 5636112 | tf_op jit(solution)/shard_map/reduce_scatter | solution.py:85
  787.8 8.3 %fusion.39 = (f32[1024,1376]{0,1:T(8,128)}, f32[1024,1376]{0,1:T(8,128)}) fusion(bf16[1024,2752]{0,1:T(8,128)(2,1)} %reduce-scatter.5.cloned.1.call-done), kind=kLoop, calls=%fused_computation.60 | loop fusion | bytes 22544384 | tf_op jit(solution)/shard_map/slice | solution.py:91
  (4 shorter events, 0.0 us)
Async XLA Ops:
  7.2 214.6 %all-gather.12.cloned.1.call-start = ((), (), s32[]{:S(2)}) async-start(), calls=%async_computation.7 | async-start | bytes 28180480 | tf_op jit(solution)/shard_map/all_gather | solution.py:65
  12.9 0.7 copy-start.9
  12.9 0.8 copy-start.4
  12.9 1.2 copy-start
  12.9 3.6 copy-start.2
  12.9 284.1 %all-gather.6.cloned.1.call-start = ((), (), s32[]{:S(2)}) async-start(), calls=%async_computation.3 | async-start | bytes 7077888 | tf_op jit(solution)/shard_map/all_gather | solution.py:59
  15.2 385.5 %all-gather.8.cloned.1.call-start = ((), (), s32[]{:S(2)}) async-start(), calls=%async_computation.4 | async-start | bytes 14090240 | tf_op jit(solution)/shard_map/all_gather | solution.py:70
  15.9 498.0 %all-gather.10.cloned.1.call-start = ((), (), s32[]{:S(2)}) async-start(), calls=%async_computation.5 | async-start | bytes 14090240 | tf_op jit(solution)/shard_map/all_gather | solution.py:71
  16.5 569.3 %reduce-scatter.3.cloned.1.call-start = ((), (), s32[]{:S(2)}) async-start(), calls=%async_computation.2 | async-start | bytes 7077888 | tf_op jit(solution)/shard_map/reduce_scatter | solution.py:73
  251.0 12.8 %copy-start.6 = (bf16[768,1376]{0,1:T(8,128)(2,1)S(1)}, bf16[768,1376]{0,1:T(8,128)(2,1)}, u32[]{:S(2)}) copy-start(bf16[768,1376]{0,1:T(8,128)(2,1)} %param.15) | copy-start | bytes 6340612
  296.3 0.7 copy-start.3
  296.4 2.1 copy-start.7
  296.4 491.4 %reduce-scatter.5.cloned.1.call-start = ((), (), s32[]{:S(2)}) async-start(), calls=%async_computation.6 | async-start | bytes 28180480 | tf_op jit(solution)/shard_map/reduce_scatter | solution.py:85
  298.5 16.4 %copy-start.5 = (bf16[768,4096]{1,0:T(8,128)(2,1)S(1)}, bf16[768,4096]{1,0:T(8,128)(2,1)}, u32[]{:S(2)}) copy-start(bf16[768,4096]{1,0:T(8,128)(2,1)} %all-gather.6.cloned.1.call-done) | copy-start | bytes 18874372
  298.5 16.4 %copy-start.8 = (bf16[768,1376]{0,1:T(8,128)(2,1)S(1)}, bf16[768,1376]{0,1:T(8,128)(2,1)}, u32[]{:S(2)}) copy-start(bf16[768,1376]{0,1:T(8,128)(2,1)} %param.21) | copy-start | bytes 6340612
  415.8 170.1 %copy-start.1 = (bf16[768,512]{1,0:T(8,128)(2,1)S(1)}, bf16[768,512]{1,0:T(8,128)(2,1)}, u32[]{:S(2)}) copy-start(bf16[768,512]{1,0:T(8,128)(2,1)} %param.16) | copy-start | bytes 2359300
Sparse Core Ops, SparseCore 0:
  13.0 208.7 all-gather.11
  224.0 64.6 all-gather.5
  290.5 110.1 all-gather.7
  402.4 111.4 all-gather.9
  516.0 69.7 reduce-scatter.2
  588.8 198.9 reduce-scatter.4
